TPU v7x, 256 devices: a whole 4x4x8 slice. The times are simulated.
256 devices in a mesh: team: 16 (over z, core), member: 16 (over x, y).
Axes of the slice: x: 4, y: 4, z: 8, core: 2. Of those that a mesh axis runs over, the one named last changes fastest.
Arguments:
- state_start: float32 [24, 1024, 2048], P(None, 'team', 'member'), may hold values from -6 to 6
- state_section: float32 [24, 1024, 2048], P(None, 'team', 'member'), may hold values from -6 to 6
- velocity: float32 [2, 1024, 2048], P(None, 'team', 'member'), may hold values from -3 to 3
- diffusivity: float32 [24], replicated, may hold values from 0.05 to 0.5
- flame_cells: int32 [256, 128], P(('team', 'member')), may hold values from 0 to 8191, as said below
- block_team: int32 [256, 1], replicated, may hold values from 0 to 15; in each aligned block of 16 rows (0 to 15, 16 to 31, ...) at most 2 rows name the same one
- w_in: bfloat16 [16, 16, 1600, 24], P('team', 'member'), may hold values from -1.25 to 1.25
- w_mid: bfloat16 [16, 16, 800, 1600], P('team', 'member'), may hold values from -0.15625 to 0.15625
- w_low: bfloat16 [16, 16, 400, 800], P('team', 'member'), may hold values from -0.21875 to 0.21875
- w_out: bfloat16 [16, 16, 24, 400], P('team', 'member'), may hold values from -0.3125 to 0.3125
Outputs:
- source_rates: float32 [24, 1024, 2048], P(None, 'team', 'member')
- new_state: float32 [24, 1024, 2048], P(None, 'team', 'member')
Inputs may be any that keep to these rules, and one draw needn't show every extreme that they name: `flame_cells`: the 128 entries of the rows of one device (rows d * 1 to d + 1 - 1) are distinct cells of that device's tile, given as i * 128 + j. `block_team`: in each aligned block of 16 rows (the flame blocks of one index of team) no regime appears more than 2 times.
All inputs are finite; a program needn't handle non-finite values.
Results may differ from a plain program's by a relative error of at most 0.0017.
The roundings to bfloat16 on the way count: a program that leaves them out, or rounds other values in their place, can miss the bound.
Values may be sent and summed in bfloat16 or wider, within the bound.
No kernel may reach another device: no remote copies, remote signals or barrier semaphores. Data moves between devices by JAX's collectives and lax.ppermute only.
A program may use at most 64 MiB of HBM per device.

v0:
```python
import jax
import jax.numpy as jnp
from jax import lax
from jax.experimental import pallas as pl
from jax.experimental.pallas import tpu as pltpu
from jax.sharding import Mesh, PartitionSpec as P


BF = jnp.bfloat16
F32 = jnp.float32
I32 = jnp.int32
TIME_STEP = 0.25
VM = pl.BlockSpec(memory_space=pltpu.VMEM)
SM = pl.BlockSpec(memory_space=pltpu.SMEM)

ANY = pl.BlockSpec(memory_space=pl.ANY)

SRC, POS, OWN, SIB, N_OWN, N_SIB = 0, 32, 48, 64, 80, 81


def dot(a, b, dims=((1,), (0,))):
    return lax.dot_general(a, b, (dims, ((), ())), preferred_element_type=F32)


def silu(x):
    return (x * lax.logistic(x)).astype(BF)


def in_hbm(array):
    return pltpu.with_memory_space_constraint(array, pltpu.HBM)


def iota(shape, dim):
    return lax.broadcasted_iota(I32, shape, dim)


def make_table(team_ref):
    z, c = lax.axis_index("z"), lax.axis_index("core")
    n = team_ref.shape[1]
    across = jnp.broadcast_to(team_ref[...].astype(F32), (n, n))
    down = across.T
    row, lane = iota((n, n), 0), iota((n, n), 1)
    before = (across == down) & (lane < row)
    rank = jnp.sum(jnp.where(before, 1.0, 0.0), axis=1, keepdims=True).astype(I32)
    shape = (n, 128)
    g = down[:, :128].astype(I32)
    rank = jnp.broadcast_to(rank, shape)
    b, s = iota(shape, 0), iota(shape, 1)
    core = (rank + g) & 1
    place = ((g >> 1) * 2 + core) * 2 + (g & 1)
    arrives = (b >> 4) * 2 + (g & 1)
    here = (b >> 4) == 2 * z + c
    own = (core == c) & (g == 2 * z + c)
    sib = (core == c) & (g == 2 * z + 1 - c)
    value = jnp.where((s < POS) & here & (place == s), b & 15, jnp.zeros(shape, I32))
    value = jnp.where((s >= POS) & (s < OWN) & here & ((b & 15) == s - POS), place, value)
    value = jnp.where((s >= OWN) & (s < SIB) & own & ((rank >> 1) == s - OWN), arrives, value)
    value = jnp.where((s >= SIB) & (s < N_OWN) & sib & ((rank >> 1) == s - SIB), arrives, value)
    value = jnp.where((s == N_OWN) & own, 1, value)
    value = jnp.where((s == N_SIB) & sib, 1, value)
    return jnp.sum(value.astype(F32), axis=0, keepdims=True).astype(I32)


def front_kernel(team_hbm, cells_hbm, state_hbm, *refs):
    table, blocks, x_low, x_high, y_low, y_high, team, cells, state, own, sems, out_sems = refs
    fields, rows, cols = state.shape
    width = cells.shape[1]
    parts = sems.shape[0] - 2
    some = fields // parts
    load_team = pltpu.make_async_copy(team_hbm, team, sems.at[parts + 1])
    load_team.start()
    loads = [pltpu.make_async_copy(cells_hbm, cells, sems.at[parts])]
    for k in range(parts):
        at = pl.ds(k * some, some)
        loads.append(pltpu.make_async_copy(state_hbm.at[at], state.at[at], sems.at[k]))
    for load in loads:
        load.start()
    loads[0].wait()
    column = cells[...] & (cols - 1)
    line = cells[...] >> (cols.bit_length() - 1)
    picks = jnp.where(iota((cols, width), 0) == column, 1.0, 0.0).astype(BF)
    at_row = (iota((rows, width), 0) == line)[None]
    e, j = iota((16, cols), 0), iota((16, cols), 1)
    ends = jnp.where(((e == 0) & (j == 0)) | ((e == 1) & (j == cols - 1)), 1.0, 0.0).astype(BF)
    load_team.wait()
    table[...] = make_table(team)
    found_in = []
    for k in range(parts):
        loads[k + 1].wait()
        values = state[k * some : (k + 1) * some].astype(BF)
        flat = values.reshape(some * rows, cols)
        found = dot(flat, picks).reshape(some, rows, width)
        found_in.append(jnp.sum(jnp.where(at_row, found, 0.0), axis=1))
    own[...] = jnp.concatenate(found_in, axis=0).astype(BF)
    sends = [pltpu.make_async_copy(own, blocks.at[k], out_sems.at[k]) for k in range(blocks.shape[0])]
    for send in sends:
        send.start()
    x_low[...] = state[:, 0, :].astype(BF)
    x_high[...] = state[:, rows - 1, :].astype(BF)
    sides = dot(ends, state[...].astype(BF).reshape(fields * rows, cols), ((1,), (1,))).astype(BF)
    y_low[...], y_high[...] = sides[0:1], sides[1:2]
    for send in sends:
        send.wait()


def select_kernel(base, table, rows, out):
    for k in range(out.shape[0]):
        out[k] = rows[table[0, base + k]]


def network_kernel(table, x, *refs):
    out, rates, sems, load_sems = refs[8], refs[9], refs[10], refs[11]
    partner, own = [refs[4], refs[5], refs[16], refs[7]], refs[12:16]
    first_load = pltpu.make_async_copy(refs[6], refs[16], load_sems.at[4])
    loads = [pltpu.make_async_copy(refs[k], own[k], load_sems.at[k]) for k in range(4)]
    for load in (first_load, *loads):
        load.start()

    def copy_of(w, p, a):
        return pltpu.make_async_copy(rates.at[w, p], out.at[a], sems.at[w, p])

    def group(weights, w, first, n, start, size, before_low=None):
        w_in, w_mid, w_low, w_out = weights
        at = [table[0, first + jnp.minimum(start + i, n - 1)] for i in range(size)]
        states = jnp.concatenate([x[i] for i in at], axis=1)
        one = silu(dot(w_in[...], states, ((0,), (0,))))
        two = silu(dot(w_mid[...], one))
        if before_low is not None:
            before_low()
        three = silu(dot(w_low[...], two))
        found = dot(w_out[...], three)
        for i, a in enumerate(at):
            rates[w, start + i] = found[:, i * 128 : (i + 1) * 128]

            @pl.when(start + i < n)
            def _(i=i, a=a):
                copy_of(w, start + i, a).start()

    counts = table[0, N_SIB], table[0, N_OWN]
    for w, (weights, first) in enumerate(((partner, SIB), (own, OWN))):
        n = counts[w]
        full = (n + 3) // 8
        if w == 0:

            @pl.when(full > 0)
            def _(n=n):
                group(partner, 0, SIB, n, 0, 8, first_load.wait)

            @pl.when(full == 0)
            def _():
                first_load.wait()

        else:
            for load in loads:
                load.wait()

        def step(k, _, weights=weights, w=w, first=first, n=n):
            group(weights, w, first, n, 8 * k, 8)
            return 0

        lax.fori_loop(1 - w, full, step, 0)

        @pl.when(n > 8 * full)
        def _(weights=weights, w=w, first=first, n=n, full=full):
            group(weights, w, first, n, 8 * full, 4)

    for w in range(2):
        for p in range(16):

            @pl.when(p < counts[w])
            def _(w=w, p=p):
                copy_of(w, p, 0).wait()


def base_kernel(diff, start, state, velocity, out):
    fields, rows, cols = state.shape
    row, lane = iota((rows, cols), 0), iota((rows, cols), 1)
    half_x, half_y = 0.5 * velocity[0], 0.5 * velocity[1]
    for f in range(fields):
        u = state[f]
        plus_x = jnp.where(row == rows - 1, 0.0, pltpu.roll(u, rows - 1, 0))
        minus_x = jnp.where(row == 0, 0.0, pltpu.roll(u, 1, 0))
        plus_y = jnp.where(lane == cols - 1, 0.0, pltpu.roll(u, cols - 1, 1))
        minus_y = jnp.where(lane == 0, 0.0, pltpu.roll(u, 1, 1))
        flow = diff[f] * (plus_x + minus_x + plus_y + minus_y - 4.0 * u)
        flow = flow - half_x * (plus_x - minus_x) - half_y * (plus_y - minus_y)
        out[f] = 0.75 * start[f] + 0.25 * (u + TIME_STEP * flow)


def final_kernel(diff, cells, parts, base, velocity, up, down, left, right, source, new, source_tile, new_tile, sems):
    fields, rows, cols = base.shape
    width = cells.shape[1]
    rates = parts[0]
    for n in range(1, parts.shape[0]):
        rates = rates + parts[n]
    high = rates.astype(BF).astype(F32)
    low = rates - high
    column = cells[...] & (cols - 1)
    line = cells[...] >> (cols.bit_length() - 1)
    at_row = iota((rows, width), 0) == line
    at_col = jnp.where(iota((cols, width), 0) == column, 1.0, 0.0).astype(BF)
    at_col = jnp.concatenate([at_col, at_col], axis=1)
    some = fields // sems.shape[1]
    copies = []
    scale = 0.25 * TIME_STEP
    e, j = iota((2, cols), 0), iota((2, cols), 1)
    ends = jnp.where(((e == 0) & (j == 0)) | ((e == 1) & (j == cols - 1)), 1.0, 0.0).astype(BF)
    edges = jnp.concatenate([left[...], right[...]], axis=0)
    sides = dot(edges, ends, ((0,), (0,))).reshape(fields, rows, cols)
    lane = iota((rows, cols), 1)
    along = jnp.where(lane == 0, 0.5, -0.5) * velocity[1]
    low_x, high_x = 0.5 * velocity[0, 0:1, :], -0.5 * velocity[0, rows - 1 : rows, :]
    for k in range(sems.shape[1]):
        spread = []
        for f in range(k * some, (k + 1) * some):
            left = jnp.where(at_row, high[f : f + 1], 0.0)
            right = jnp.where(at_row, low[f : f + 1], 0.0)
            spread.append(jnp.concatenate([left, right], axis=1).astype(BF))
        placed = dot(jnp.concatenate(spread, axis=0), at_col, ((1,), (1,)))
        placed = placed.reshape(some, rows, cols)
        part = pl.ds(k * some, some)
        source_tile[part] = placed
        for f in range(some):
            g = k * some + f
            new_tile[g] = base[g] + scale * (placed[f] + (diff[g] + along) * sides[g])
            above, below = up[g : g + 1].astype(F32), down[g : g + 1].astype(F32)
            new_tile[g, 0:1] = new_tile[g, 0:1] + scale * (diff[g] + low_x) * above
            new_tile[g, rows - 1 : rows] = new_tile[g, rows - 1 : rows] + scale * (diff[g] + high_x) * below
        for i, (tile, out) in enumerate(((source_tile, source), (new_tile, new))):
            copies.append(pltpu.make_async_copy(tile.at[part], out.at[part], sems.at[i, k]))
            copies[-1].start()
    for copy in copies:
        copy.wait()


def call(body, out_shape, in_specs, out_specs=None, scratch=(), mib=8):
    if out_specs is None:
        out_specs = jax.tree.map(lambda _: VM, out_shape)
    return pl.pallas_call(
        body, out_shape=out_shape, in_specs=in_specs, out_specs=out_specs,
        scratch_shapes=scratch, compiler_params=pltpu.CompilerParams(vmem_limit_bytes=mib * 2**20),
    )


def shards(start, state, velocity, diffusivity, cells, block_team, w_in, w_mid, w_low, w_out):
    fields, rows, cols = state.shape
    width = cells.shape[1]
    sds = jax.ShapeDtypeStruct
    members = lax.axis_size("member")
    teams = lax.axis_size("z") * lax.axis_size("core")
    up = [(i, (i + 1) % 16) for i in range(16)]
    back = [(b, a) for a, b in up]
    swap = [(0, 1), (1, 0)]
    line = ("z", "core")

    weights = [w_in[0, 0].T, w_mid[0, 0], w_low[0, 0], w_out[0, 0]]
    edge = sds((1, fields * rows), BF)
    team = block_team.T
    table, blocks, x_low, x_high, y_low, y_high = call(
        front_kernel,
        (sds((1, 128), I32), sds((members, fields, width), BF), sds((fields, cols), BF), sds((fields, cols), BF), edge, edge),
        [ANY] * 3, (VM, ANY, VM, VM, VM, VM),
        scratch=[pltpu.VMEM(team.shape, I32), pltpu.VMEM(cells.shape, I32), pltpu.VMEM(state.shape, F32), pltpu.VMEM((fields, width), BF),
                 pltpu.SemaphoreType.DMA((5,)), pltpu.SemaphoreType.DMA((members,))],
    )(in_hbm(team), in_hbm(cells), in_hbm(state))
    blocks, *sent = lax.optimization_barrier((blocks, *weights))
    gathered = lax.all_to_all(blocks, "member", 0, 0, tiled=True)
    partner = [lax.ppermute(sent[k], "core", swap) for k in (0, 3)]
    partner[1:1] = [lax.ppermute(sent[k], "core", swap) for k in (1, 2)]
    gathered, partner[0], partner[3] = lax.optimization_barrier((gathered, partner[0], partner[3]))
    outgoing = call(lambda *r: select_kernel(SRC, *r), sds((2 * teams, fields, width), BF), [SM, VM])(table, gathered)
    incoming = lax.all_to_all(outgoing, line, 0, 0, tiled=True)

    produced = call(
        network_kernel, sds((2 * teams, fields, width), F32), [SM, VM] + [ANY] * 4 + [VM, VM, ANY, VM], ANY,
        scratch=[pltpu.VMEM((2, 16, fields, width), F32), pltpu.SemaphoreType.DMA((2, 16)), pltpu.SemaphoreType.DMA((5,))]
        + [pltpu.VMEM(w.shape, BF) for w in (*weights, weights[2])],
        mib=32,
    )(table, incoming, *[in_hbm(w) for w in weights], partner[0], partner[1], in_hbm(partner[2]), partner[3])
    produced, x_low, x_high, y_low, y_high = lax.optimization_barrier((produced, x_low, x_high, y_low, y_high))
    returned = lax.all_to_all(produced, line, 0, 0, tiled=True)
    halos = (
        lax.ppermute(x_high, line, up),
        lax.ppermute(x_low, line, back),
        lax.ppermute(y_high, "member", up),
        lax.ppermute(y_low, "member", back),
    )
    base = call(base_kernel, sds(state.shape, F32), [SM] + [VM] * 3)(
        diffusivity, in_hbm(start), in_hbm(state), in_hbm(velocity)
    )
    returned, base, *halos = lax.optimization_barrier((returned, base, *halos))
    terms = call(lambda *r: select_kernel(POS, *r), sds((members, fields, width), F32), [SM, VM])(table, returned)
    parts = lax.all_to_all(terms, "member", 0, 0, tiled=True)
    return call(
        final_kernel, (sds(state.shape, F32), sds(state.shape, F32)), [SM] + [VM] * 8, (ANY, ANY),
        scratch=[pltpu.VMEM(state.shape, F32), pltpu.VMEM(state.shape, F32), pltpu.SemaphoreType.DMA((2, 3))],
    )(diffusivity, cells, parts, base, velocity, *halos)


def solution(mesh):
    team, member = mesh.devices.shape
    own_mesh = Mesh(mesh.devices.reshape(team // 2, 2, member), ("z", "core", "member"))
    line = ("z", "core")
    tile = P(None, line, "member")
    weight = P(line, "member", None, None)
    return jax.shard_map(
        shards,
        mesh=own_mesh,
        in_specs=(tile, tile, tile, P(), P((*line, "member"), None), P(), weight, weight, weight, weight),
        out_specs=(tile, tile),
        check_vma=False,
    )
```

profile of v0, /device:TPU:1, one launch (start us, length us, event | category | flops | bytes accessed | tf_op | source)
XLA Modules:
  0.0 87.4 jit_solution(1382709006750373798)
XLA Ops:
  0.6 2.5 %shard_map.113 = (s32[1,128]{1,0:T(1,128)S(1)}, bf16[16,24,128]{2,1,0:T(8,128)(2,1)}, bf16[24,128]{1,0:T(8,128)(2,1)S(1)}, bf16[24,128]{1,0:T(8,128)(2,1)S(1)}, ...) custom-call(s32[1,256]{1,0:T(1,128)} %bitcast.15, s32[1,128]{1,0:T(1,128)} %cells.1, f32[24,64,128]{2,1,0:T(8,128)} %state.1), custom_call_target="tpu_custom_call" | custom-call | tf_op jit(solution)/shard_map/pallas_call | solution.py:259
  3.1 3.3 %collective-permute-start.2 = (bf16[800,1600]{1,0:T(8,128)(2,1)}, bf16[800,1600]{1,0:T(8,128)(2,1)S(1)}, u32[]{:S(2)}, u32[]{:S(2)}) collective-permute-start(bf16[800,1600]{1,0:T(8,128)(2,1)} %bitcast.7), channel_id=1, source_target_pairs={{0,16},{16,0},{1,17},{17,1},{2,18},{18,2},{3,19},{19,3},{4,20},{20... | collective-permute-start | bytes 7680008 | tf_op jit(solution)/shard_map/ppermute | solution.py:269
  6.4 0.1 collective-permute-start.3
  6.5 5.0 %all-to-all-start = ((bf16[16,24,128]{2,1,0:T(8,128)(2,1)}), bf16[16,24,128]{2,1,0:T(8,128)(2,1)S(1)}, u32[]{:S(2)}, u32[]{:S(2)}) async-start(bf16[16,24,128]{2,1,0:T(8,128)(2,1)} %get-tuple-element.29), calls=%async_computation | async-start | bytes 196608 | tf_op jit(solution)/shard_map/all_to_all | solution.py:267
  11.6 0.8 collective-permute-start
  12.4 0.1 collective-permute-start.1
  12.5 1.3 %collective-permute-done.1.refs_7_ = bf16[24,400]{1,0:T(8,128)(2,1)S(1)} collective-permute-done((bf16[24,400]{1,0:T(8,128)(2,1)}, bf16[24,400]{1,0:T(8,128)(2,1)S(1)}, u32[]{:S(2)}, u32[]{:S(2)}) %collective-permute-start.1) | collective-permute-done | bytes 19232 | tf_op jit(solution)/shard_map/ppermute | solution.py:268
  13.8 0.0 collective-permute-done.refs_4_
  13.8 4.4 %all-to-all-done.r_1_ = bf16[16,24,128]{2,1,0:T(8,128)(2,1)S(1)} async-done(((bf16[16,24,128]{2,1,0:T(8,128)(2,1)}), bf16[16,24,128]{2,1,0:T(8,128)(2,1)S(1)}, u32[]{:S(2)}, u32[]{:S(2)}) %all-to-all-start) | async-done | bytes 98336 | tf_op jit(solution)/shard_map/all_to_all | solution.py:267
  18.2 0.6 shard_map.114
  18.8 20.3 %all_to_all.20.x = bf16[32,24,128]{2,1,0:T(8,128)(2,1)S(1)} all-to-all(bf16[32,24,128]{2,1,0:T(8,128)(2,1)S(1)} %shard_map.114), channel_id=1, replica_groups=mesh['z'=8,'core'=2,'member'=16] {'z','core'}, dimensions={0} | all-to-all | bytes 393216 | tf_op jit(solution)/shard_map/all_to_all | solution.py:272
  39.1 0.0 copy-start.2
  39.1 0.0 collective-permute-done.3.refs_6_
  39.1 0.0 collective-permute-done.2.refs_5_
  39.1 11.9 %shard_map.115 = f32[32,24,128]{2,1,0:T(8,128)} custom-call(s32[1,128]{1,0:T(1,128)S(1)} %get-tuple-element.27.r_0_.table, bf16[32,24,128]{2,1,0:T(8,128)(2,1)S(1)} %all_to_all.20.x, bf16[24,1600]{1,0:T(8,128)(2,1)} %bitcast.12, bf16[800,1600]{1,0:T(8,128)(2,1)} %bitcast.8, bf16[400,800]{1,0:T(8,128)(2,1)} %bitcast.10, bf16[24,400]{1,0:T(8,128)(2,1)} %bitcast.14, ...), custom_call_target="tpu_custom_call" | custom-call | tf_op jit(solution)/shard_map/pallas_call | solution.py:274
  51.0 0.0 copy-start
  51.0 0.0 copy-start.1
  51.0 8.1 %all-to-all-start.2 = ((f32[32,24,128]{2,1,0:T(8,128)}), f32[32,24,128]{2,1,0:T(8,128)S(1)}, u32[]{:S(2)}, u32[]{:S(2)}) async-start(f32[32,24,128]{2,1,0:T(8,128)} %shard_map.115), calls=%async_computation.2 | async-start | bytes 786432 | tf_op jit(solution)/shard_map/all_to_all | solution.py:281
  59.1 1.6 %collective-permute-start.4 = (bf16[24,128]{1,0:T(8,128)(2,1)S(1)}, bf16[24,128]{1,0:T(8,128)(2,1)S(1)}, u32[]{:S(2)}, u32[]{:S(2)}) collective-permute-start(bf16[24,128]{1,0:T(8,128)(2,1)S(1)} %get-tuple-element.42), channel_id=1, source_target_pairs={{0,16},{16,32},{32,48},{48,64},{64,80},{80,96},{96,112},{112,128},... | collective-permute-start | bytes 18440 | tf_op jit(solution)/shard_map/ppermute | solution.py:283
  60.8 0.0 collective-permute-start.5
  60.8 0.2 collective-permute-start.6
  61.0 4.5 %collective-permute-start.7 = (bf16[1,1536]{1,0:T(2,128)(2,1)S(1)}, bf16[1,1536]{1,0:T(2,128)(2,1)S(1)}, u32[]{:S(2)}, u32[]{:S(2)}) collective-permute-start(bf16[1,1536]{1,0:T(2,128)(2,1)S(1)} %get-tuple-element.45), channel_id=1, source_target_pairs={{1,0},{2,1},{3,2},{4,3},{5,4},{6,5},{7,6},{8,7},{9,8},{10,9},{11,1... | collective-permute-start | bytes 9224 | tf_op jit(solution)/shard_map/ppermute | solution.py:286
  65.5 0.0 copy-done.2
  65.5 2.1 %shard_map.116.base = f32[24,64,128]{2,1,0:T(8,128)S(1)} custom-call(f32[24]{0:T(128)S(1)} %copy-done.2, f32[24,64,128]{2,1,0:T(8,128)} %start.1, f32[24,64,128]{2,1,0:T(8,128)} %state.1, f32[2,64,128]{2,1,0:T(8,128)} %velocity.3), custom_call_target="tpu_custom_call" | custom-call | tf_op jit(solution)/shard_map/pallas_call | solution.py:288
  67.6 0.0 collective-permute-done.6.left
  67.6 0.0 collective-permute-done.7.right
  67.6 0.0 collective-permute-done.4.up
  67.7 2.8 %collective-permute-done.5.down = bf16[24,128]{1,0:T(8,128)(2,1)S(1)} collective-permute-done((bf16[24,128]{1,0:T(8,128)(2,1)S(1)}, bf16[24,128]{1,0:T(8,128)(2,1)S(1)}, u32[]{:S(2)}, u32[]{:S(2)}) %collective-permute-start.5) | collective-permute-done | bytes 6176 | tf_op jit(solution)/shard_map/ppermute | solution.py:284
  70.5 3.2 %all-to-all-done.2.r_1_ = f32[32,24,128]{2,1,0:T(8,128)S(1)} async-done(((f32[32,24,128]{2,1,0:T(8,128)}), f32[32,24,128]{2,1,0:T(8,128)S(1)}, u32[]{:S(2)}, u32[]{:S(2)}) %all-to-all-start.2) | async-done | bytes 393248 | tf_op jit(solution)/shard_map/all_to_all | solution.py:281
  73.6 0.6 shard_map.117
  74.2 10.9 %all_to_all.21.parts = f32[16,24,128]{2,1,0:T(8,128)S(1)} all-to-all(f32[16,24,128]{2,1,0:T(8,128)S(1)} %shard_map.117), channel_id=1, replica_groups=mesh['z'=8,'core'=2,'member'=16] {'member'}, dimensions={0} | all-to-all | bytes 393216 | tf_op jit(solution)/shard_map/all_to_all | solution.py:293
  85.2 0.0 copy-done
  85.2 0.0 copy-done.1
  85.2 2.1 %shard_map.118 = (f32[24,64,128]{2,1,0:T(8,128)}, f32[24,64,128]{2,1,0:T(8,128)}) custom-call(f32[24]{0:T(128)S(1)} %copy-done.2, s32[1,128]{1,0:T(1,128)S(1)} %copy-done.1, f32[16,24,128]{2,1,0:T(8,128)S(1)} %all_to_all.21.parts, f32[24,64,128]{2,1,0:T(8,128)S(1)} %shard_map.116.base, f32[2,64,128]{2,1,0:T(8,128)S(1)} %copy-done, ...), custom_call_target="tpu_custom_call" | custom-call | tf_op jit(solution)/shard_map/pallas_call | solution.py:294
Async XLA Ops:
  3.1 35.9 %collective-permute-start.2 = (bf16[800,1600]{1,0:T(8,128)(2,1)}, bf16[800,1600]{1,0:T(8,128)(2,1)S(1)}, u32[]{:S(2)}, u32[]{:S(2)}) collective-permute-start(bf16[800,1600]{1,0:T(8,128)(2,1)} %bitcast.7), channel_id=1, source_target_pairs={{0,16},{16,0},{1,17},{17,1},{2,18},{18,2},{3,19},{19,3},{4,20},{20... | collective-permute-start | bytes 7680008 | tf_op jit(solution)/shard_map/ppermute | solution.py:269
  6.4 32.7 %collective-permute-start.3 = (bf16[400,800]{1,0:T(8,128)(2,1)}, bf16[400,800]{1,0:T(8,128)(2,1)}, u32[]{:S(2)}, u32[]{:S(2)}) collective-permute-start(bf16[400,800]{1,0:T(8,128)(2,1)} %bitcast.9), channel_id=1, source_target_pairs={{0,16},{16,0},{1,17},{17,1},{2,18},{18,2},{3,19},{19,3},{4,20},{20... | collective-permute-start | bytes 1920008 | tf_op jit(solution)/shard_map/ppermute | solution.py:269
  6.5 11.7 %all-to-all-start = ((bf16[16,24,128]{2,1,0:T(8,128)(2,1)}), bf16[16,24,128]{2,1,0:T(8,128)(2,1)S(1)}, u32[]{:S(2)}, u32[]{:S(2)}) async-start(bf16[16,24,128]{2,1,0:T(8,128)(2,1)} %get-tuple-element.29), calls=%async_computation | async-start | bytes 196608 | tf_op jit(solution)/shard_map/all_to_all | solution.py:267
  11.6 2.2 %collective-permute-start = (bf16[24,1600]{1,0:T(8,128)(2,1)}, bf16[24,1600]{1,0:T(8,128)(2,1)S(1)}, u32[]{:S(2)}, u32[]{:S(2)}) collective-permute-start(bf16[24,1600]{1,0:T(8,128)(2,1)} %bitcast.11), channel_id=1, source_target_pairs={{0,16},{16,0},{1,17},{17,1},{2,18},{18,2},{3,19},{19,3},{4,20},{20... | collective-permute-start | bytes 230408 | tf_op jit(solution)/shard_map/ppermute | solution.py:268
  12.4 1.4 %collective-permute-start.1 = (bf16[24,400]{1,0:T(8,128)(2,1)}, bf16[24,400]{1,0:T(8,128)(2,1)S(1)}, u32[]{:S(2)}, u32[]{:S(2)}) collective-permute-start(bf16[24,400]{1,0:T(8,128)(2,1)} %bitcast.13), channel_id=1, source_target_pairs={{0,16},{16,0},{1,17},{17,1},{2,18},{18,2},{3,19},{19,3},{4,20},{20... | collective-permute-start | bytes 57608 | tf_op jit(solution)/shard_map/ppermute | solution.py:268
  39.1 26.5 %copy-start.2 = (f32[24]{0:T(128)S(1)}, f32[24]{0:T(128)}, u32[]{:S(2)}) copy-start(f32[24]{0:T(128)} %diff.3) | copy-start | bytes 292
  51.0 34.2 %copy-start = (f32[2,64,128]{2,1,0:T(8,128)S(1)}, f32[2,64,128]{2,1,0:T(8,128)}, u32[]{:S(2)}) copy-start(f32[2,64,128]{2,1,0:T(8,128)} %velocity.3) | copy-start | bytes 196612
  51.0 34.2 %copy-start.1 = (s32[1,128]{1,0:T(1,128)S(1)}, s32[1,128]{1,0:T(1,128)}, u32[]{:S(2)}) copy-start(s32[1,128]{1,0:T(1,128)} %cells.1) | copy-start | bytes 1540
  51.0 22.7 %all-to-all-start.2 = ((f32[32,24,128]{2,1,0:T(8,128)}), f32[32,24,128]{2,1,0:T(8,128)S(1)}, u32[]{:S(2)}, u32[]{:S(2)}) async-start(f32[32,24,128]{2,1,0:T(8,128)} %shard_map.115), calls=%async_computation.2 | async-start | bytes 786432 | tf_op jit(solution)/shard_map/all_to_all | solution.py:281
  59.1 8.5 %collective-permute-start.4 = (bf16[24,128]{1,0:T(8,128)(2,1)S(1)}, bf16[24,128]{1,0:T(8,128)(2,1)S(1)}, u32[]{:S(2)}, u32[]{:S(2)}) collective-permute-start(bf16[24,128]{1,0:T(8,128)(2,1)S(1)} %get-tuple-element.42), channel_id=1, source_target_pairs={{0,16},{16,32},{32,48},{48,64},{64,80},{80,96},{96,112},{112,128},... | collective-permute-start | bytes 18440 | tf_op jit(solution)/shard_map/ppermute | solution.py:283
  60.8 9.7 %collective-permute-start.5 = (bf16[24,128]{1,0:T(8,128)(2,1)S(1)}, bf16[24,128]{1,0:T(8,128)(2,1)S(1)}, u32[]{:S(2)}, u32[]{:S(2)}) collective-permute-start(bf16[24,128]{1,0:T(8,128)(2,1)S(1)} %get-tuple-element.43), channel_id=1, source_target_pairs={{16,0},{32,16},{48,32},{64,48},{80,64},{96,80},{112,96},{128,112},... | collective-permute-start | bytes 18440 | tf_op jit(solution)/shard_map/ppermute | solution.py:284
  60.8 6.9 %collective-permute-start.6 = (bf16[1,1536]{1,0:T(2,128)(2,1)S(1)}, bf16[1,1536]{1,0:T(2,128)(2,1)S(1)}, u32[]{:S(2)}, u32[]{:S(2)}) collective-permute-start(bf16[1,1536]{1,0:T(2,128)(2,1)S(1)} %get-tuple-element.44), channel_id=1, source_target_pairs={{0,1},{1,2},{2,3},{3,4},{4,5},{5,6},{6,7},{7,8},{8,9},{9,10},{10,1... | collective-permute-start | bytes 9224 | tf_op jit(solution)/shard_map/ppermute | solution.py:285
  61.0 6.6 %collective-permute-start.7 = (bf16[1,1536]{1,0:T(2,128)(2,1)S(1)}, bf16[1,1536]{1,0:T(2,128)(2,1)S(1)}, u32[]{:S(2)}, u32[]{:S(2)}) collective-permute-start(bf16[1,1536]{1,0:T(2,128)(2,1)S(1)} %get-tuple-element.45), channel_id=1, source_target_pairs={{1,0},{2,1},{3,2},{4,3},{5,4},{6,5},{7,6},{8,7},{9,8},{10,9},{11,1... | collective-permute-start | bytes 9224 | tf_op jit(solution)/shard_map/ppermute | solution.py:286
where the time goes:
time: 87.8 us; the launch traced here: 87.4 us
  blocking collectives  31.3 us (36%)
  starting transfers between devices  23.9 us (27%)
  Pallas kernels  19.7 us (22%)
  waiting for transfers between devices  11.7 us (13%)
  between operations  0.89 us (1%)
    all_to_all x1, blocking collectives, shards(): incoming = lax.all_to_all(outgoing, line, 0, 0, tiled=True)  20.3 us
    pallas_call x1, Pallas kernels, shards(): call(network_kernel, sds((2 * teams, fields, width), F32), [SM, VM] + [AN...  11.9 us
    all_to_all x1, blocking collectives, shards(): parts = lax.all_to_all(terms, 'member', 0, 0, tiled=True)  10.9 us
    all_to_all x1, starting transfers between devices, shards(): returned = lax.all_to_all(produced, line, 0, 0, tiled=True)  8.14 us
    all_to_all x1, starting transfers between devices, shards(): gathered = lax.all_to_all(blocks, 'member', 0, 0, tiled=True)  5.05 us
    ppermute x1, starting transfers between devices, shards(): lax.ppermute(y_low, 'member', back)  4.54 us
    all_to_all x1, waiting for transfers between devices, shards(): gathered = lax.all_to_all(blocks, 'member', 0, 0, tiled=True)  4.41 us
    ppermute x2, starting transfers between devices, shards(): partner[1:1] = [lax.ppermute(sent[k], 'core', swap) for k in (1, 2)]  3.39 us
  transfers between devices with their start and end apart: 10, of which 4 were waited for; matrix products, arithmetic and copies ran while one was open for 0% of the time, Pallas kernels for 3%

commit v1 on v0

--- a/solution.py
+++ b/solution.py
@@ -124,7 +124,8 @@
         at = [table[0, first + jnp.minimum(start + i, n - 1)] for i in range(size)]
         states = jnp.concatenate([x[i] for i in at], axis=1)
         one = silu(dot(w_in[...], states, ((0,), (0,))))
-        two = silu(dot(w_mid[...], one))
+        half = w_mid.shape[0] // 2
+        two = jnp.concatenate([silu(dot(w_mid[:half], one)), silu(dot(w_mid[half:], one))], axis=0)
         if before_low is not None:
             before_low()
         three = silu(dot(w_low[...], two))
@@ -172,7 +173,7 @@
                 copy_of(w, p, 0).wait()
 
 
-def base_kernel(diff, start, state, velocity, out):
+def base_kernel(diff, start, state, velocity, out, spread):
     fields, rows, cols = state.shape
     row, lane = iota((rows, cols), 0), iota((rows, cols), 1)
     half_x, half_y = 0.5 * velocity[0], 0.5 * velocity[1]
@@ -185,6 +186,7 @@
         flow = diff[f] * (plus_x + minus_x + plus_y + minus_y - 4.0 * u)
         flow = flow - half_x * (plus_x - minus_x) - half_y * (plus_y - minus_y)
         out[f] = 0.75 * start[f] + 0.25 * (u + TIME_STEP * flow)
+        spread[f : f + 1] = jnp.full((1, cols), diff[f], F32)
 
 
 def final_kernel(diff, cells, parts, base, velocity, up, down, left, right, source, new, source_tile, new_tile, sems):
@@ -222,10 +224,10 @@
         source_tile[part] = placed
         for f in range(some):
             g = k * some + f
-            new_tile[g] = base[g] + scale * (placed[f] + (diff[g] + along) * sides[g])
+            new_tile[g] = base[g] + scale * (placed[f] + (diff[g : g + 1] + along) * sides[g])
             above, below = up[g : g + 1].astype(F32), down[g : g + 1].astype(F32)
-            new_tile[g, 0:1] = new_tile[g, 0:1] + scale * (diff[g] + low_x) * above
-            new_tile[g, rows - 1 : rows] = new_tile[g, rows - 1 : rows] + scale * (diff[g] + high_x) * below
+            new_tile[g, 0:1] = new_tile[g, 0:1] + scale * (diff[g : g + 1] + low_x) * above
+            new_tile[g, rows - 1 : rows] = new_tile[g, rows - 1 : rows] + scale * (diff[g : g + 1] + high_x) * below
         for i, (tile, out) in enumerate(((source_tile, source), (new_tile, new))):
             copies.append(pltpu.make_async_copy(tile.at[part], out.at[part], sems.at[i, k]))
             copies[-1].start()
@@ -285,16 +287,16 @@
         lax.ppermute(y_high, "member", up),
         lax.ppermute(y_low, "member", back),
     )
-    base = call(base_kernel, sds(state.shape, F32), [SM] + [VM] * 3)(
+    base, spread = call(base_kernel, (sds(state.shape, F32), sds((fields, cols), F32)), [SM] + [VM] * 3)(
         diffusivity, in_hbm(start), in_hbm(state), in_hbm(velocity)
     )
     returned, base, *halos = lax.optimization_barrier((returned, base, *halos))
     terms = call(lambda *r: select_kernel(POS, *r), sds((members, fields, width), F32), [SM, VM])(table, returned)
     parts = lax.all_to_all(terms, "member", 0, 0, tiled=True)
     return call(
-        final_kernel, (sds(state.shape, F32), sds(state.shape, F32)), [SM] + [VM] * 8, (ANY, ANY),
-        scratch=[pltpu.VMEM(state.shape, F32), pltpu.VMEM(state.shape, F32), pltpu.SemaphoreType.DMA((2, 3))],
-    )(diffusivity, cells, parts, base, velocity, *halos)
+        final_kernel, (sds(state.shape, F32), sds(state.shape, F32)), [VM] * 9, (ANY, ANY),
+        scratch=[pltpu.VMEM(state.shape, F32), pltpu.VMEM(state.shape, F32), pltpu.SemaphoreType.DMA((2, 4))],
+    )(spread, cells, parts, base, velocity, *halos)
 
 
 def solution(mesh):

time: 87.8 us -> 87.1 us (level)
  no operation moved by 1% of the time
where the time goes in v1:
time: 87.1 us; the launch traced here: 86.7 us
  blocking collectives  31.3 us (36%)
  starting transfers between devices  23.9 us (27%)
  Pallas kernels  19 us (22%)
  waiting for transfers between devices  11.7 us (13%)
  between operations  0.89 us (1%)
    all_to_all x1, blocking collectives, shards(): incoming = lax.all_to_all(outgoing, line, 0, 0, tiled=True)  20.3 us
    pallas_call x1, Pallas kernels, shards(): call(network_kernel, sds((2 * teams, fields, width), F32), [SM, VM] + [AN...  11.8 us
    all_to_all x1, blocking collectives, shards(): parts = lax.all_to_all(terms, 'member', 0, 0, tiled=True)  10.9 us
    all_to_all x1, starting transfers between devices, shards(): returned = lax.all_to_all(produced, line, 0, 0, tiled=True)  8.12 us
    all_to_all x1, starting transfers between devices, shards(): gathered = lax.all_to_all(blocks, 'member', 0, 0, tiled=True)  5.05 us
    ppermute x1, starting transfers between devices, shards(): lax.ppermute(y_low, 'member', back)  4.54 us
    all_to_all x1, waiting for transfers between devices, shards(): gathered = lax.all_to_all(blocks, 'member', 0, 0, tiled=True)  4.41 us
    ppermute x2, starting transfers between devices, shards(): partner[1:1] = [lax.ppermute(sent[k], 'core', swap) for k in (1, 2)]  3.39 us
  transfers between devices with their start and end apart: 10, of which 4 were waited for; matrix products, arithmetic and copies ran while one was open for 0% of the time, Pallas kernels for 3%

profile of v1, /device:TPU:1, one launch (start us, length us, event | category | flops | bytes accessed | tf_op | source)
XLA Modules:
  0.0 86.7 jit_solution(1867258547237192154)
XLA Ops:
  0.6 2.5 %shard_map.114 = (s32[1,128]{1,0:T(1,128)S(1)}, bf16[16,24,128]{2,1,0:T(8,128)(2,1)}, bf16[24,128]{1,0:T(8,128)(2,1)S(1)}, bf16[24,128]{1,0:T(8,128)(2,1)S(1)}, ...) custom-call(s32[1,256]{1,0:T(1,128)} %bitcast.15, s32[1,128]{1,0:T(1,128)} %cells.1, f32[24,64,128]{2,1,0:T(8,128)} %state_hbm.1), custom_call_target="tpu_custom_call" | custom-call | tf_op jit(solution)/shard_map/pallas_call | solution.py:261
  3.1 3.3 %collective-permute-start.2 = (bf16[800,1600]{1,0:T(8,128)(2,1)}, bf16[800,1600]{1,0:T(8,128)(2,1)S(1)}, u32[]{:S(2)}, u32[]{:S(2)}) collective-permute-start(bf16[800,1600]{1,0:T(8,128)(2,1)} %bitcast.7), channel_id=1, source_target_pairs={{0,16},{16,0},{1,17},{17,1},{2,18},{18,2},{3,19},{19,3},{4,20},{20... | collective-permute-start | bytes 7680008 | tf_op jit(solution)/shard_map/ppermute | solution.py:271
  6.4 0.1 collective-permute-start.3
  6.5 5.0 %all-to-all-start = ((bf16[16,24,128]{2,1,0:T(8,128)(2,1)}), bf16[16,24,128]{2,1,0:T(8,128)(2,1)S(1)}, u32[]{:S(2)}, u32[]{:S(2)}) async-start(bf16[16,24,128]{2,1,0:T(8,128)(2,1)} %get-tuple-element.32), calls=%async_computation | async-start | bytes 196608 | tf_op jit(solution)/shard_map/all_to_all | solution.py:269
  11.6 0.8 collective-permute-start
  12.4 0.1 collective-permute-start.1
  12.5 1.3 %collective-permute-done.1.refs_7_ = bf16[24,400]{1,0:T(8,128)(2,1)S(1)} collective-permute-done((bf16[24,400]{1,0:T(8,128)(2,1)}, bf16[24,400]{1,0:T(8,128)(2,1)S(1)}, u32[]{:S(2)}, u32[]{:S(2)}) %collective-permute-start.1) | collective-permute-done | bytes 19232 | tf_op jit(solution)/shard_map/ppermute | solution.py:270
  13.8 0.0 collective-permute-done.refs_4_
  13.8 4.4 %all-to-all-done.r_1_ = bf16[16,24,128]{2,1,0:T(8,128)(2,1)S(1)} async-done(((bf16[16,24,128]{2,1,0:T(8,128)(2,1)}), bf16[16,24,128]{2,1,0:T(8,128)(2,1)S(1)}, u32[]{:S(2)}, u32[]{:S(2)}) %all-to-all-start) | async-done | bytes 98336 | tf_op jit(solution)/shard_map/all_to_all | solution.py:269
  18.2 0.6 shard_map.115
  18.8 20.3 %all_to_all.20.x = bf16[32,24,128]{2,1,0:T(8,128)(2,1)S(1)} all-to-all(bf16[32,24,128]{2,1,0:T(8,128)(2,1)S(1)} %shard_map.115), channel_id=1, replica_groups=mesh['z'=8,'core'=2,'member'=16] {'z','core'}, dimensions={0} | all-to-all | bytes 393216 | tf_op jit(solution)/shard_map/all_to_all | solution.py:274
  39.1 0.0 copy-start.2
  39.1 0.0 collective-permute-done.3.refs_6_
  39.1 0.0 collective-permute-done.2.refs_5_
  39.1 11.8 %shard_map.116 = f32[32,24,128]{2,1,0:T(8,128)} custom-call(s32[1,128]{1,0:T(1,128)S(1)} %get-tuple-element.30.r_0_.table, bf16[32,24,128]{2,1,0:T(8,128)(2,1)S(1)} %all_to_all.20.x, bf16[24,1600]{1,0:T(8,128)(2,1)} %bitcast.12, bf16[800,1600]{1,0:T(8,128)(2,1)} %bitcast.8, bf16[400,800]{1,0:T(8,128)(2,1)} %bitcast.10, bf16[24,400]{1,0:T(8,128)(2,1)} %bitcast.14, ...), custom_call_target="tpu_custom_call" | custom-call | tf_op jit(solution)/shard_map/pallas_call | solution.py:276
  50.9 0.0 copy-start
  50.9 0.0 copy-start.1
  50.9 8.1 %all-to-all-start.2 = ((f32[32,24,128]{2,1,0:T(8,128)}), f32[32,24,128]{2,1,0:T(8,128)S(1)}, u32[]{:S(2)}, u32[]{:S(2)}) async-start(f32[32,24,128]{2,1,0:T(8,128)} %shard_map.116), calls=%async_computation.2 | async-start | bytes 786432 | tf_op jit(solution)/shard_map/all_to_all | solution.py:283
  59.0 1.6 %collective-permute-start.4 = (bf16[24,128]{1,0:T(8,128)(2,1)S(1)}, bf16[24,128]{1,0:T(8,128)(2,1)S(1)}, u32[]{:S(2)}, u32[]{:S(2)}) collective-permute-start(bf16[24,128]{1,0:T(8,128)(2,1)S(1)} %get-tuple-element.46), channel_id=1, source_target_pairs={{0,16},{16,32},{32,48},{48,64},{64,80},{80,96},{96,112},{112,128},... | collective-permute-start | bytes 18440 | tf_op jit(solution)/shard_map/ppermute | solution.py:285
  60.6 0.0 collective-permute-start.5
  60.6 0.2 collective-permute-start.6
  60.9 4.5 %collective-permute-start.7 = (bf16[1,1536]{1,0:T(2,128)(2,1)S(1)}, bf16[1,1536]{1,0:T(2,128)(2,1)S(1)}, u32[]{:S(2)}, u32[]{:S(2)}) collective-permute-start(bf16[1,1536]{1,0:T(2,128)(2,1)S(1)} %get-tuple-element.49), channel_id=1, source_target_pairs={{1,0},{2,1},{3,2},{4,3},{5,4},{6,5},{7,6},{8,7},{9,8},{10,9},{11,1... | collective-permute-start | bytes 9224 | tf_op jit(solution)/shard_map/ppermute | solution.py:288
  65.4 0.0 copy-done.2
  65.4 2.1 %shard_map.113 = (f32[24,64,128]{2,1,0:T(8,128)S(1)}, f32[24,128]{1,0:T(8,128)S(1)}) custom-call(f32[24]{0:T(128)S(1)} %copy-done.2, f32[24,64,128]{2,1,0:T(8,128)} %start.1, f32[24,64,128]{2,1,0:T(8,128)} %state_hbm.1, f32[2,64,128]{2,1,0:T(8,128)} %velocity.3), custom_call_target="tpu_custom_call" | custom-call | tf_op jit(solution)/shard_map/pallas_call | solution.py:290
  67.5 0.0 collective-permute-done.6.left
  67.5 0.0 collective-permute-done.7.right
  67.5 0.0 collective-permute-done.4.up
  67.5 2.8 %collective-permute-done.5.down = bf16[24,128]{1,0:T(8,128)(2,1)S(1)} collective-permute-done((bf16[24,128]{1,0:T(8,128)(2,1)S(1)}, bf16[24,128]{1,0:T(8,128)(2,1)S(1)}, u32[]{:S(2)}, u32[]{:S(2)}) %collective-permute-start.5) | collective-permute-done | bytes 6176 | tf_op jit(solution)/shard_map/ppermute | solution.py:286
  70.3 3.2 %all-to-all-done.2.r_1_ = f32[32,24,128]{2,1,0:T(8,128)S(1)} async-done(((f32[32,24,128]{2,1,0:T(8,128)}), f32[32,24,128]{2,1,0:T(8,128)S(1)}, u32[]{:S(2)}, u32[]{:S(2)}) %all-to-all-start.2) | async-done | bytes 393248 | tf_op jit(solution)/shard_map/all_to_all | solution.py:283
  73.5 0.6 shard_map.117
  74.1 10.9 %all_to_all.21.parts = f32[16,24,128]{2,1,0:T(8,128)S(1)} all-to-all(f32[16,24,128]{2,1,0:T(8,128)S(1)} %shard_map.117), channel_id=1, replica_groups=mesh['z'=8,'core'=2,'member'=16] {'member'}, dimensions={0} | all-to-all | bytes 393216 | tf_op jit(solution)/shard_map/all_to_all | solution.py:295
  85.0 0.0 copy-done
  85.0 0.0 copy-done.1
  85.1 1.5 %shard_map.118 = (f32[24,64,128]{2,1,0:T(8,128)}, f32[24,64,128]{2,1,0:T(8,128)}) custom-call(f32[24,128]{1,0:T(8,128)S(1)} %get-tuple-element.29.diff, s32[1,128]{1,0:T(1,128)S(1)} %copy-done.1, f32[16,24,128]{2,1,0:T(8,128)S(1)} %all_to_all.21.parts, f32[24,64,128]{2,1,0:T(8,128)S(1)} %get-tuple-element.51.base, f32[2,64,128]{2,1,0:T(8,128)S(1)} %copy-done, ...), custom_call_target="tpu_custom_call" | custom-call | tf_op jit(solution)/shard_map/pallas_call | solution.py:296
Async XLA Ops:
  3.1 35.9 %collective-permute-start.2 = (bf16[800,1600]{1,0:T(8,128)(2,1)}, bf16[800,1600]{1,0:T(8,128)(2,1)S(1)}, u32[]{:S(2)}, u32[]{:S(2)}) collective-permute-start(bf16[800,1600]{1,0:T(8,128)(2,1)} %bitcast.7), channel_id=1, source_target_pairs={{0,16},{16,0},{1,17},{17,1},{2,18},{18,2},{3,19},{19,3},{4,20},{20... | collective-permute-start | bytes 7680008 | tf_op jit(solution)/shard_map/ppermute | solution.py:271
  6.4 32.7 %collective-permute-start.3 = (bf16[400,800]{1,0:T(8,128)(2,1)}, bf16[400,800]{1,0:T(8,128)(2,1)}, u32[]{:S(2)}, u32[]{:S(2)}) collective-permute-start(bf16[400,800]{1,0:T(8,128)(2,1)} %bitcast.9), channel_id=1, source_target_pairs={{0,16},{16,0},{1,17},{17,1},{2,18},{18,2},{3,19},{19,3},{4,20},{20... | collective-permute-start | bytes 1920008 | tf_op jit(solution)/shard_map/ppermute | solution.py:271
  6.5 11.7 %all-to-all-start = ((bf16[16,24,128]{2,1,0:T(8,128)(2,1)}), bf16[16,24,128]{2,1,0:T(8,128)(2,1)S(1)}, u32[]{:S(2)}, u32[]{:S(2)}) async-start(bf16[16,24,128]{2,1,0:T(8,128)(2,1)} %get-tuple-element.32), calls=%async_computation | async-start | bytes 196608 | tf_op jit(solution)/shard_map/all_to_all | solution.py:269
  11.6 2.2 %collective-permute-start = (bf16[24,1600]{1,0:T(8,128)(2,1)}, bf16[24,1600]{1,0:T(8,128)(2,1)S(1)}, u32[]{:S(2)}, u32[]{:S(2)}) collective-permute-start(bf16[24,1600]{1,0:T(8,128)(2,1)} %bitcast.11), channel_id=1, source_target_pairs={{0,16},{16,0},{1,17},{17,1},{2,18},{18,2},{3,19},{19,3},{4,20},{20... | collective-permute-start | bytes 230408 | tf_op jit(solution)/shard_map/ppermute | solution.py:270
  12.4 1.4 %collective-permute-start.1 = (bf16[24,400]{1,0:T(8,128)(2,1)}, bf16[24,400]{1,0:T(8,128)(2,1)S(1)}, u32[]{:S(2)}, u32[]{:S(2)}) collective-permute-start(bf16[24,400]{1,0:T(8,128)(2,1)} %bitcast.13), channel_id=1, source_target_pairs={{0,16},{16,0},{1,17},{17,1},{2,18},{18,2},{3,19},{19,3},{4,20},{20... | collective-permute-start | bytes 57608 | tf_op jit(solution)/shard_map/ppermute | solution.py:270
  39.1 26.4 %copy-start.2 = (f32[24]{0:T(128)S(1)}, f32[24]{0:T(128)}, u32[]{:S(2)}) copy-start(f32[24]{0:T(128)} %diff.1) | copy-start | bytes 292
  50.9 34.2 %copy-start = (f32[2,64,128]{2,1,0:T(8,128)S(1)}, f32[2,64,128]{2,1,0:T(8,128)}, u32[]{:S(2)}) copy-start(f32[2,64,128]{2,1,0:T(8,128)} %velocity.3) | copy-start | bytes 196612
  50.9 34.2 %copy-start.1 = (s32[1,128]{1,0:T(1,128)S(1)}, s32[1,128]{1,0:T(1,128)}, u32[]{:S(2)}) copy-start(s32[1,128]{1,0:T(1,128)} %cells.1) | copy-start | bytes 1540
  50.9 22.6 %all-to-all-start.2 = ((f32[32,24,128]{2,1,0:T(8,128)}), f32[32,24,128]{2,1,0:T(8,128)S(1)}, u32[]{:S(2)}, u32[]{:S(2)}) async-start(f32[32,24,128]{2,1,0:T(8,128)} %shard_map.116), calls=%async_computation.2 | async-start | bytes 786432 | tf_op jit(solution)/shard_map/all_to_all | solution.py:283
  59.0 8.5 %collective-permute-start.4 = (bf16[24,128]{1,0:T(8,128)(2,1)S(1)}, bf16[24,128]{1,0:T(8,128)(2,1)S(1)}, u32[]{:S(2)}, u32[]{:S(2)}) collective-permute-start(bf16[24,128]{1,0:T(8,128)(2,1)S(1)} %get-tuple-element.46), channel_id=1, source_target_pairs={{0,16},{16,32},{32,48},{48,64},{64,80},{80,96},{96,112},{112,128},... | collective-permute-start | bytes 18440 | tf_op jit(solution)/shard_map/ppermute | solution.py:285
  60.6 9.7 %collective-permute-start.5 = (bf16[24,128]{1,0:T(8,128)(2,1)S(1)}, bf16[24,128]{1,0:T(8,128)(2,1)S(1)}, u32[]{:S(2)}, u32[]{:S(2)}) collective-permute-start(bf16[24,128]{1,0:T(8,128)(2,1)S(1)} %get-tuple-element.47), channel_id=1, source_target_pairs={{16,0},{32,16},{48,32},{64,48},{80,64},{96,80},{112,96},{128,112},... | collective-permute-start | bytes 18440 | tf_op jit(solution)/shard_map/ppermute | solution.py:286
  60.6 6.9 %collective-permute-start.6 = (bf16[1,1536]{1,0:T(2,128)(2,1)S(1)}, bf16[1,1536]{1,0:T(2,128)(2,1)S(1)}, u32[]{:S(2)}, u32[]{:S(2)}) collective-permute-start(bf16[1,1536]{1,0:T(2,128)(2,1)S(1)} %get-tuple-element.48), channel_id=1, source_target_pairs={{0,1},{1,2},{2,3},{3,4},{4,5},{5,6},{6,7},{7,8},{8,9},{9,10},{10,1... | collective-permute-start | bytes 9224 | tf_op jit(solution)/shard_map/ppermute | solution.py:287
  60.9 6.6 %collective-permute-start.7 = (bf16[1,1536]{1,0:T(2,128)(2,1)S(1)}, bf16[1,1536]{1,0:T(2,128)(2,1)S(1)}, u32[]{:S(2)}, u32[]{:S(2)}) collective-permute-start(bf16[1,1536]{1,0:T(2,128)(2,1)S(1)} %get-tuple-element.49), channel_id=1, source_target_pairs={{1,0},{2,1},{3,2},{4,3},{5,4},{6,5},{7,6},{8,7},{9,8},{10,9},{11,1... | collective-permute-start | bytes 9224 | tf_op jit(solution)/shard_map/ppermute | solution.py:288
